TPU v7x, 64 devices: a 2x2x8 block of a 4x4x8 slice. The times are simulated.
64 devices in a mesh: kv: 4 (over x, y), dup: 16 (over z, core).
Axes of the slice: x: 2, y: 2, z: 8, core: 2. Of those that a mesh axis runs over, the one named last changes fastest.
The devices are a block of a 4x4x8 slice.
Arguments:
- queries: bfloat16 [1024, 64, 128], P('kv', 'dup'), parts along dimension 0
- key_cache: bfloat16 [1024, 2048, 128], P('kv', 'dup'), parts along dimension 0
- value_cache: bfloat16 [1024, 2048, 128], P('kv', 'dup'), parts along dimension 0
- lengths: int32 [1024], P('kv'), parts along dimension 0
Outputs:
- output: bfloat16 [1024, 64, 128], P('kv', 'dup'), parts along dimension 0
There are 4 independent parts. A program takes and returns all parts, laid end to end along the dimension named above; each array names one.
All inputs are finite; a program needn't handle non-finite values.
Results may differ from a plain program's by a relative error of at most 0.00814941.
Values are sent between devices in bfloat16 or wider.
A program may use at most 768 MiB of HBM per device.

v0:
```python
import jax
import jax.numpy as jnp
from jax import lax
from jax.sharding import PartitionSpec as P, NamedSharding

DRAFT = 4
NEG_BIG = -1e30


def solution(mesh):
    dup_size = mesh.shape["dup"]

    def group_step(q_local, k_span, v_span, len_local):
        num_batch, span_len, head_dim = k_span.shape
        span_start = lax.axis_index("dup") * span_len
        q_group = lax.all_gather(q_local, "dup", axis=1, tiled=True)
        num_rows = q_group.shape[1]
        own_rows = num_rows // dup_size
        scores = jnp.einsum("brd,bsd->brs", q_group, k_span, preferred_element_type=jnp.float32) * (head_dim ** -0.5)
        last_pos = len_local[:, None] - DRAFT + (jnp.arange(num_rows) % DRAFT)[None, :]
        allowed = (span_start + jnp.arange(span_len))[None, None, :] <= last_pos[:, :, None]
        scores = jnp.where(allowed, scores, NEG_BIG)
        row_peak = jnp.max(scores, axis=2, keepdims=True)
        prob_vals = jnp.exp(scores - row_peak)
        row_mass = jnp.sum(prob_vals, axis=2, keepdims=True)
        weighted = jnp.einsum("brs,bsd->brd", prob_vals.astype(jnp.bfloat16), v_span, preferred_element_type=jnp.float32)
        part_out = (weighted / row_mass).astype(jnp.bfloat16).reshape(num_batch, dup_size, own_rows, head_dim)
        log_mass = (row_peak + jnp.log(row_mass)).reshape(num_batch, dup_size, own_rows)
        recv_out = lax.all_to_all(part_out, "dup", 1, 1)
        recv_mass = lax.all_to_all(log_mass, "dup", 1, 1)
        top_mass = jnp.max(recv_mass, axis=1, keepdims=True)
        weights = jnp.exp(recv_mass - top_mass)
        total_mass = jnp.sum(weights, axis=1)
        merged = jnp.sum(weights[..., None] * recv_out.astype(jnp.float32), axis=1)
        return (merged / total_mass[..., None]).astype(jnp.bfloat16)

    return jax.shard_map(group_step, mesh=mesh, in_specs=(P("kv", "dup", None), P("kv", "dup", None), P("kv", "dup", None), P("kv")), out_specs=P("kv", "dup", None), check_vma=False)
```

profile of v0, /device:TPU:21, one launch (start us, length us, event | category | flops | bytes accessed | tf_op | source)
XLA Modules:
  0.0 210.3 jit_solution(6235656446367544120)
XLA Ops:
  6.5 0.0 all-gather.2.cloned.1.call-start
  6.6 1.7 copy.8
  8.2 0.1 all-gather.2.cloned.1.call-update
  8.3 0.7 broadcast_add_fusion.1
  9.0 0.1 broadcast_add_fusion
  9.1 43.6 %all-gather.2.cloned.1.call-done = bf16[256,64,128]{2,0,1:T(8,128)(2,1)} async-done(((bf16[256,4,128]{2,0,1:T(8,128)(2,1)}), bf16[256,64,128]{2,0,1:T(8,128)(2,1)}) %all-gather.2.cloned.1.call-update) | async-done | bytes 4194320 | tf_op jit(solution)/shard_map/all_gather | solution.py:16
  52.7 10.3 %fusion.2 = (f32[256,64]{1,0:T(8,128)S(1)}, f32[256,64,128]{2,1,0:T(8,128)S(1)}) fusion(s32[256,64]{1,0:T(8,128)S(1)} %broadcast_add_fusion, s32[128]{0:T(128)S(1)} %iota_add_fusion, bf16[256,128,128]{2,1,0:T(8,128)(2,1)} %param.5, bf16[256,64,128]{2,0,1:T(8,128)(2,1)} %all-gather.2.cloned.1.call-done), kind=kOutput, calls=%fused_computation.6 | convolution fusion | flops 545243136 | bytes 21103104 | tf_op jit(solution)/shard_map/brd,bsd->brs/dot_general | solution.py:19
  63.0 0.0 copy-start
  63.0 3.2 %copy-done = f32[256,64,128]{2,1,0:T(8,128)} copy-done((f32[256,64,128]{2,1,0:T(8,128)}, f32[256,64,128]{2,1,0:T(8,128)S(1)}, u32[]{:S(2)}) %copy-start) | copy-done | bytes 8388632
  66.2 8.4 %fusion.1 = f32[256,64]{1,0:T(8,128)S(1)} fusion(f32[256,64,128]{2,1,0:T(8,128)S(1)} %get-tuple-element.8, f32[256,64]{1,0:T(8,128)S(1)} %get-tuple-element.7, s32[256,64]{1,0:T(8,128)S(1)} %broadcast_add_fusion, s32[128]{0:T(128)S(1)} %iota_add_fusion), kind=kLoop, calls=%fused_computation.5 | loop fusion | flops 10469376 | bytes 8585728 | tf_op jit(solution)/shard_map/reduce_sum | solution.py:25
  74.6 0.1 copy.10
  74.7 0.7 add.55
  75.3 4.4 %all-to-all-start = ((f32[256,16,4]{0,2,1:T(4,128)}), f32[256,16,4]{0,2,1:T(4,128)S(1)}, u32[]{:S(2)}, u32[]{:S(2)}) async-start(f32[256,16,4]{0,2,1:T(4,128)} %add.55), calls=%async_computation | async-start | bytes 131072 | tf_op jit(solution)/shard_map/all_to_all | solution.py:30
  79.7 11.1 %divide_convert_fusion = bf16[256,64,128]{2,1,0:T(8,128)(2,1)S(1)} fusion(f32[256,64]{1,0:T(8,128)S(1)} %fusion.1, bf16[256,128,128]{2,1,0:T(8,128)(2,1)} %param.6, f32[256,64,128]{2,1,0:T(8,128)} %copy-done, f32[256,64]{1,0:T(8,128)S(1)} %get-tuple-element.7, s32[256,64]{1,0:T(8,128)S(1)} %broadcast_add_fusion, s32[128]{0:T(128)S(1)} %iota_add_fusion), kind=kOutput, calls=%fused_computation.1 | convolution fusion | flops 551550976 | bytes 21168640 | tf_op jit(solution)/shard_map/brs,bsd->brd/dot_general | solution.py:26
  90.8 4.0 %copy.12 = bf16[256,16,4,128]{3,2,0,1:T(4,128)(2,1)} copy(bf16[256,16,4,128]{3,2,1,0:T(4,128)(2,1)S(1)} %bitcast.5) | data formatting | bytes 8388608 | tf_op jit(solution)/shard_map/reshape | solution.py:27
  94.8 0.0 all-to-all-done
  94.8 7.2 %all-to-all-start.1 = ((bf16[256,16,4,128]{3,2,0,1:T(4,128)(2,1)}), bf16[256,16,4,128]{3,2,0,1:T(4,128)(2,1)}, u32[]{:S(2)}, u32[]{:S(2)}) async-start(bf16[256,16,4,128]{3,2,0,1:T(4,128)(2,1)} %copy.12), calls=%async_computation.1 | async-start | bytes 8388608 | tf_op jit(solution)/shard_map/all_to_all | solution.py:29
  102.1 0.1 copy.13
  102.3 0.6 copy.11
  102.9 91.9 %all-to-all-done.1 = bf16[256,16,4,128]{3,2,0,1:T(4,128)(2,1)} async-done(((bf16[256,16,4,128]{3,2,0,1:T(4,128)(2,1)}), bf16[256,16,4,128]{3,2,0,1:T(4,128)(2,1)}, u32[]{:S(2)}, u32[]{:S(2)}) %all-to-all-start.1) | async-done | bytes 4194336 | tf_op jit(solution)/shard_map/all_to_all | solution.py:29
  194.8 7.5 %multiply_reduce_fusion = f32[256,4,128]{2,1,0:T(4,128)S(1)} fusion(bf16[256,16,4,128]{3,2,0,1:T(4,128)(2,1)} %all-to-all-done.1, f32[256,16,4]{2,0,1:T(8,128)S(1)} %copy.11), kind=kLoop, calls=%fused_computation | loop fusion | flops 6160384 | bytes 4784128 | tf_op jit(solution)/shard_map/reduce_sum | solution.py:34
  202.4 1.0 divide_convert_fusion.1
  (5 shorter events, 0.1 us)
Async XLA Ops:
  6.5 46.1 %all-gather.2.cloned.1.call-start = ((), (), s32[]{:S(2)}) async-start(), calls=%async_computation.2 | async-start | bytes 4456448 | tf_op jit(solution)/shard_map/all_gather | solution.py:16
  63.0 3.2 %copy-start = (f32[256,64,128]{2,1,0:T(8,128)}, f32[256,64,128]{2,1,0:T(8,128)S(1)}, u32[]{:S(2)}) copy-start(f32[256,64,128]{2,1,0:T(8,128)S(1)} %get-tuple-element.8) | copy-start | bytes 25165828
  75.3 19.5 %all-to-all-start = ((f32[256,16,4]{0,2,1:T(4,128)}), f32[256,16,4]{0,2,1:T(4,128)S(1)}, u32[]{:S(2)}, u32[]{:S(2)}) async-start(f32[256,16,4]{0,2,1:T(4,128)} %add.55), calls=%async_computation | async-start | bytes 131072 | tf_op jit(solution)/shard_map/all_to_all | solution.py:30
  94.8 100.0 %all-to-all-start.1 = ((bf16[256,16,4,128]{3,2,0,1:T(4,128)(2,1)}), bf16[256,16,4,128]{3,2,0,1:T(4,128)(2,1)}, u32[]{:S(2)}, u32[]{:S(2)}) async-start(bf16[256,16,4,128]{3,2,0,1:T(4,128)(2,1)} %copy.12), calls=%async_computation.1 | async-start | bytes 8388608 | tf_op jit(solution)/shard_map/all_to_all | solution.py:29
Sparse Core Ops, SparseCore 0:
  9.0 43.6 all-gather.1
where the time goes:
time: 211 us; the launch traced here: 210 us
  waiting for transfers between devices  136 us (64%)
  matrix products  21.4 us (10%)
  other arithmetic  17.8 us (8%)
  between operations  13.5 us (6%)
  starting transfers between devices  11.6 us (5%)
  local copies, waits for them, and re-layouts  10.4 us (5%)
    all_to_all x1, waiting for transfers between devices, group_step(): recv_out = lax.all_to_all(part_out, 'dup', 1, 1)  91.9 us
    all_gather x1, waiting for transfers between devices, group_step(): q_group = lax.all_gather(q_local, 'dup', axis=1, tiled=True)  43.6 us
    dot_general x1, matrix products, group_step(): jnp.einsum('brs,bsd->brd', prob_vals.astype(jnp.bfloat16), v_span, prefer...  11.1 us
    dot_general x1, matrix products, group_step(): jnp.einsum('brd,bsd->brs', q_group, k_span, preferred_element_type=jnp.fl...  10.3 us
    reduce_sum x1, other arithmetic, group_step(): row_mass = jnp.sum(prob_vals, axis=2, keepdims=True)  8.37 us
    reduce_sum x1, other arithmetic, group_step(): merged = jnp.sum(weights[..., None] * recv_out.astype(jnp.float32), axis=1)  7.54 us
    all_to_all x1, starting transfers between devices, group_step(): recv_out = lax.all_to_all(part_out, 'dup', 1, 1)  7.24 us
    unnamed x3, local copies, waits for them, and re-layouts  4.9 us
  transfers between devices with their start and end apart: 3, of which 2 were waited for; matrix products, arithmetic and copies ran while one was open for 8% of the time, Pallas kernels for 0%

commit v1 on v0

v1 whole, which is shorter than its diff:
```python
import functools
import math

import jax
import jax.numpy as jnp
from jax import lax
from jax.experimental import pallas as pl
from jax.experimental.pallas import tpu as pltpu
from jax.sharding import PartitionSpec as P

DRAFT = 4
NEG_BIG = -1e30
LANES = 128
GROUP = 16
MESH_ID = pl.DeviceIdType.MESH

SKEW_GATHER = (0, 1, 2, 3, 4)
SKEW_COMPUTE = 5
SKEW_REDUCE = (10, 9, 8, 7, 6)


def kernel(ring, len_ref, q_hbm, k_hbm, v_hbm, out_hbm,
           q_all, o_all, o_pair, o_in, o_half, s_all, s_pair, s_in, k_buf, v_buf, out_buf, s_acc,
           q_sem, k_sem, v_sem, out_sem, ag_send, ag_recv, pq_send, pq_recv,
           po_send, po_recv, ps_send, ps_recv, rs_send, rs_recv, ss_send, ss_recv):
    half = ring // 2
    num_chunks = s_all.shape[1]
    rows = LANES
    half_rows = rows // 2
    seqs = rows // DRAFT
    head_dim = q_hbm.shape[-1]
    span_len = k_hbm.shape[1]

    me = lax.axis_index("dup")
    z = me // 2
    core = lax.rem(me, 2)
    partner = me + 1 - 2 * core
    right = lax.rem(z + 1, ring) * 2 + core
    left = lax.rem(z + ring - 1, ring) * 2 + core
    beside = (right, left)

    def load_kv(c):
        span = pl.ds(c * seqs, seqs)
        return (pltpu.make_async_copy(k_hbm.at[span], k_buf.at[span], k_sem.at[c]),
                pltpu.make_async_copy(v_hbm.at[span], v_buf.at[span], v_sem.at[c]))

    load_q = pltpu.make_async_copy(q_hbm, q_all.at[0, 0], q_sem)
    load_q.start()

    barrier = pltpu.get_barrier_semaphore()
    for other in (right, left, partner):
        pl.semaphore_signal(barrier, inc=1, device_id={"dup": other}, device_id_type=MESH_ID)

    @pl.loop(0, num_chunks)
    def _(c):
        for copy in load_kv(c):
            copy.start()

    load_q.wait()
    pl.semaphore_wait(barrier, 3)

    def send(src, dst, send_sem, recv_sem, other):
        return pltpu.make_async_remote_copy(src_ref=src, dst_ref=dst, send_sem=send_sem, recv_sem=recv_sem,
                                            device_id={"dup": other}, device_id_type=MESH_ID)

    def arrived(ref, sem):
        pltpu.make_async_copy(ref, ref, sem).wait()

    def chunk_rows(c):
        return pl.ds(pl.multiple_of(c * rows, rows), rows)

    def split_rows(c, way):
        return pl.ds(pl.multiple_of(c * rows + way * half_rows, half_rows), half_rows)

    def half_rows_of(c):
        return pl.ds(pl.multiple_of(c * half_rows, half_rows), half_rows)

    def slot_at(way, hop):
        return lax.rem(ring - hop, ring) if way == 0 else hop

    def gather(hop, c):
        area = chunk_rows(c)
        slots = [(ring - hop) % ring, hop % ring]
        if 0 < hop < half:
            for way in range(2):
                arrived(q_all.at[0, slots[way], area], ag_recv.at[c, way, hop - 1])
        elif hop == half:
            for way in range(2):
                arrived(q_all.at[0, half, split_rows(c, way)], ag_recv.at[c, way, hop - 1])
        if hop < half:
            for way in range(2):
                part = area if hop + 1 < half else split_rows(c, way)
                to = (ring - hop - 1) if way == 0 else hop + 1
                send(q_all.at[0, slots[way], part], q_all.at[0, to, part],
                     ag_send.at[way, hop], ag_recv.at[c, way, hop], beside[way]).start()
        for slot in sorted(set(slots)):
            send(q_all.at[0, slot, area], q_all.at[1, slot, area], pq_send, pq_recv.at[c], partner).start()

    sub = lax.broadcasted_iota(jnp.int32, (8, LANES), 0)
    lane = lax.broadcasted_iota(jnp.int32, (8, LANES), 1)
    low = (sub < DRAFT)[None]
    lane_less_token = lane - lax.rem(sub, DRAFT)
    scale = math.log2(math.e) / math.sqrt(head_dim)

    def compute(c):
        area = chunk_rows(c)
        arrived(q_all.at[1, :, area], pq_recv.at[c])
        for copy in load_kv(c):
            copy.wait()
        s_acc[...] = jnp.zeros_like(s_acc)

        @pl.loop(0, seqs // GROUP)
        def _(g):
            first = g * GROUP
            r0 = pl.multiple_of(c * rows + first * DRAFT, GROUP * DRAFT)
            q = q_all[:, :, pl.ds(r0, GROUP * DRAFT), :].astype(jnp.float32)
            q = q.reshape(2, ring, GROUP // 2, 8, head_dim)
            acc = s_acc[...]
            outs = []
            for pair in range(GROUP // 2):
                mine, theirs = q[0, :, pair], q[1, :, pair]
                both = (jnp.where(low, mine, pltpu.roll(theirs, DRAFT, 1)), jnp.where(low, pltpu.roll(mine, DRAFT, 1), theirs))
                pair_out = []
                for odd in range(2):
                    local = first + 2 * pair + odd
                    seq = c * seqs + local
                    q_rows = both[odd].reshape(ring * 8, head_dim).astype(jnp.bfloat16)
                    s = lax.dot_general(q_rows, k_buf[seq], (((1,), (1,)), ((), ())), preferred_element_type=jnp.float32)
                    limit = len_ref[seq] - DRAFT - me * span_len
                    s = jnp.where((lane_less_token <= limit)[None], s.reshape(ring, 8, span_len), NEG_BIG)
                    peak = jnp.max(s, axis=2, keepdims=True)
                    p = jnp.exp2((s - peak) * scale)
                    mass = jnp.sum(p, axis=2, keepdims=True)
                    o = jnp.dot(p.astype(jnp.bfloat16).reshape(ring * 8, span_len), v_buf[seq], preferred_element_type=jnp.float32)
                    pair_out.append(o.reshape(ring, 8, head_dim) * (1.0 / mass))
                    log_mass = peak * scale + jnp.log2(mass)
                    acc = jnp.where((lane_less_token == DRAFT * local)[None], log_mass, acc)
                even, odd_ = pair_out
                outs.append((jnp.where(low, even, pltpu.roll(odd_, DRAFT, 1)), jnp.where(low, pltpu.roll(even, DRAFT, 1), odd_)))
                if pair % 2 == 1:
                    at = pl.ds(pl.multiple_of(r0 + (pair - 1) * 8, 16), 16)
                    for side in range(2):
                        tile = jnp.concatenate([outs[-2][side], outs[-1][side]], axis=1)
                        o_all[side, :, at, :] = tile.astype(jnp.bfloat16)
            s_acc[...] = acc

        acc = s_acc[...]
        mine = jnp.sum(jnp.where(low, acc, 0.0), axis=1)
        theirs = jnp.sum(jnp.where(low, 0.0, acc), axis=1)
        for slot in range(ring):
            s_all[0, c, slot] = mine[slot:slot + 1]
            s_all[1, c, slot] = theirs[slot:slot + 1]
        send(o_all.at[1, :, area], o_pair.at[:, area], po_send, po_recv.at[c], partner).start()
        send(s_all.at[1, c], s_pair.at[c], ps_send, ps_recv.at[c], partner).start()

    def weigh(stats):
        top = functools.reduce(jnp.maximum, stats)
        parts = [jnp.exp2(s - top) for s in stats]
        total = functools.reduce(jnp.add, parts)
        inv = 1.0 / total
        cols = [jnp.broadcast_to(p * inv, (LANES, LANES)).T for p in parts]
        return cols, top + jnp.log2(total)

    def mix(cols, blocks):
        return functools.reduce(jnp.add, [w * b.astype(jnp.float32) for w, b in zip(cols, blocks)])

    row_lane = lax.broadcasted_iota(jnp.int32, (1, LANES), 1)

    def reduce_hop(dist, c):
        area = chunk_rows(c)
        if dist == half:
            arrived(o_pair.at[:, area], po_recv.at[c])
            arrived(s_pair.at[c], ps_recv.at[c])
            cols, stat = weigh([s_all[0, c, half], s_pair[c, half]])
            o_all[0, half, area, :] = mix(cols, [o_all[0, half, area, :], o_pair[half, area, :]]).astype(jnp.bfloat16)
            s_all[0, c, half] = stat
            for way in range(2):
                send(o_all.at[0, half, split_rows(c, way)], o_half.at[way, half_rows_of(c)],
                     rs_send.at[way, half - 1], rs_recv.at[c, way, half - 1], beside[way]).start()
                send(s_all.at[0, c, half], s_in.at[way, half - 1, c],
                     ss_send.at[way, half - 1], ss_recv.at[c, way, half - 1], beside[way]).start()
            return
        for way in range(2):
            if dist == half - 1:
                arrived(o_half.at[way, half_rows_of(c)], rs_recv.at[c, way, dist])
            else:
                arrived(o_in.at[way, dist, area], rs_recv.at[c, way, dist])
            arrived(s_in.at[way, dist, c], ss_recv.at[c, way, dist])
            if dist == 0:
                continue
            slot = dist if way == 0 else ring - dist
            coming = s_in[way, dist, c]
            if dist == half - 1:
                coming = jnp.where((row_lane < half_rows) if way == 0 else (row_lane >= half_rows), coming, NEG_BIG)
            cols, stat = weigh([s_all[0, c, slot], s_pair[c, slot], coming])
            if dist == half - 1:
                for part in range(2):
                    at = split_rows(c, part)
                    blocks = [o_all[0, slot, at, :], o_pair[slot, at, :]]
                    if part == way:
                        blocks.append(o_half[way, half_rows_of(c), :])
                    cut = [w[part * half_rows:(part + 1) * half_rows] for w in cols]
                    o_all[0, slot, at, :] = mix(cut, blocks).astype(jnp.bfloat16)
            else:
                blocks = [o_all[0, slot, area, :], o_pair[slot, area, :], o_in[way, dist, area, :]]
                o_all[0, slot, area, :] = mix(cols, blocks).astype(jnp.bfloat16)
            s_all[0, c, slot] = stat
            send(o_all.at[0, slot, area], o_in.at[way, dist - 1, area],
                 rs_send.at[way, dist - 1], rs_recv.at[c, way, dist - 1], beside[way]).start()
            send(s_all.at[0, c, slot], s_in.at[way, dist - 1, c],
                 ss_send.at[way, dist - 1], ss_recv.at[c, way, dist - 1], beside[way]).start()
        if dist == 0:
            cols, _ = weigh([s_all[0, c, 0], s_pair[c, 0], s_in[0, 0, c], s_in[1, 0, c]])
            blocks = [o_all[0, 0, area, :], o_pair[0, area, :], o_in[0, 0, area, :], o_in[1, 0, area, :]]
            out_buf[area, :] = mix(cols, blocks).astype(jnp.bfloat16)
            pltpu.make_async_copy(out_buf.at[area], out_hbm.at[area], out_sem).start()

    stages = [(SKEW_GATHER[hop], functools.partial(gather, hop)) for hop in reversed(range(half + 1))]
    stages += [(SKEW_COMPUTE, compute)]
    stages += [(SKEW_REDUCE[dist], functools.partial(reduce_hop, dist)) for dist in range(half + 1)]

    @pl.loop(0, num_chunks + max(skew for skew, _ in stages))
    def _(step):
        for skew, stage in stages:
            c = step - skew

            @pl.when(jnp.logical_and(c >= 0, c < num_chunks))
            def _(stage=stage, c=c):
                stage(c)

    for way in range(2):
        for hop in range(half):
            area = pl.ds(0, num_chunks * (rows if hop + 1 < half else half_rows))
            arrived(q_all.at[0, hop, area], ag_send.at[way, hop])
            arrived(o_all.at[0, hop, area], rs_send.at[way, hop])
            arrived(s_in.at[way, hop], ss_send.at[way, hop])
    arrived(q_all.at[1], pq_send)
    arrived(o_all.at[1], po_send)
    arrived(s_all.at[1], ps_send)
    arrived(out_buf, out_sem)


def solution(mesh):
    dup_size = mesh.shape["dup"]
    ring = dup_size // 2
    half = ring // 2

    def group_step(q_local, k_span, v_span, len_local):
        num_batch, draft, head_dim = q_local.shape
        total_rows = num_batch * draft
        chunks = total_rows // LANES
        bf16, f32 = jnp.bfloat16, jnp.float32
        dma = pltpu.SemaphoreType.DMA
        out = pl.pallas_call(
            functools.partial(kernel, ring),
            out_shape=jax.ShapeDtypeStruct((total_rows, head_dim), bf16),
            in_specs=[pl.BlockSpec(memory_space=pltpu.SMEM)] + [pl.BlockSpec(memory_space=pl.ANY)] * 3,
            out_specs=pl.BlockSpec(memory_space=pl.ANY),
            scratch_shapes=[
                pltpu.VMEM((2, ring, total_rows, head_dim), bf16),
                pltpu.VMEM((2, ring, total_rows, head_dim), bf16),
                pltpu.VMEM((ring, total_rows, head_dim), bf16),
                pltpu.VMEM((2, half - 1, total_rows, head_dim), bf16),
                pltpu.VMEM((2, total_rows // 2, head_dim), bf16),
                pltpu.VMEM((2, chunks, ring, 1, LANES), f32),
                pltpu.VMEM((chunks, ring, 1, LANES), f32),
                pltpu.VMEM((2, half, chunks, 1, LANES), f32),
                pltpu.VMEM(k_span.shape, bf16),
                pltpu.VMEM(v_span.shape, bf16),
                pltpu.VMEM((total_rows, head_dim), bf16),
                pltpu.VMEM((ring, 8, LANES), f32),
                dma, dma((chunks,)), dma((chunks,)), dma,
                dma((2, half)), dma((chunks, 2, half)), dma, dma((chunks,)),
                dma, dma((chunks,)), dma, dma((chunks,)),
                dma((2, half)), dma((chunks, 2, half)), dma((2, half)), dma((chunks, 2, half)),
            ],
            compiler_params=pltpu.CompilerParams(collective_id=0, has_side_effects=True, vmem_limit_bytes=60 * 1024 * 1024),
        )(len_local, q_local.reshape(total_rows, head_dim), k_span, v_span)
        return out.reshape(num_batch, draft, head_dim)

    return jax.shard_map(group_step, mesh=mesh, in_specs=(P("kv", "dup", None), P("kv", "dup", None), P("kv", "dup", None), P("kv")), out_specs=P("kv", "dup", None), check_vma=False)
```

time: 211 us -> 125 us (0.59)
  the two profiles are of different devices: /device:TPU:21 before, /device:TPU:22 now
where the time goes in v1:
time: 125 us
  Pallas kernels  123 us (98%)
  local copies, waits for them, and re-layouts  1.74 us (1%)
    pallas_call x1, Pallas kernels, group_step(): pl.pallas_call(functools.partial(kernel, ring), out_shape=jax.ShapeDtypeS...  123 us

profile of v1, /device:TPU:22, one launch (start us, length us, event | category | flops | bytes accessed | tf_op | source)
XLA Modules:
  0.0 125.0 jit_solution(12203365634125695166)
XLA Ops:
  0.0 123.2 %shard_map.46 = bf16[1024,128]{1,0:T(8,128)(2,1)} custom-call(s32[256]{0:T(256)} %len_ref.1, bf16[1024,128]{1,0:T(8,128)(2,1)} %bitcast.3, bf16[256,128,128]{2,1,0:T(8,128)(2,1)} %k_hbm.1, bf16[256,128,128]{2,1,0:T(8,128)(2,1)} %v_hbm.1), custom_call_target="tpu_custom_call" | custom-call | tf_op jit(solution)/shard_map/pallas_call | solution.py:254
  123.3 1.7 %copy.6 = bf16[256,4,128]{2,1,0:T(4,128)(2,1)} copy(bf16[256,4,128]{2,1,0:T(4,128)(2,1)} %bitcast.2) | data formatting | bytes 524288

commit v2 on v1

--- a/solution.py
+++ b/solution.py
@@ -11,16 +11,17 @@
 DRAFT = 4
 NEG_BIG = -1e30
 LANES = 128
-GROUP = 16
+QUAD = 4
+LAG = 1
 MESH_ID = pl.DeviceIdType.MESH
 
-SKEW_GATHER = (0, 1, 2, 3, 4)
-SKEW_COMPUTE = 5
-SKEW_REDUCE = (10, 9, 8, 7, 6)
+SKEW_GATHER = (0, 2, 4, 6, 8)
+SKEW_COMPUTE = 9
+SKEW_REDUCE = (18, 16, 14, 12, 10)
 
 
 def kernel(ring, len_ref, q_hbm, k_hbm, v_hbm, out_hbm,
-           q_all, o_all, o_pair, o_in, o_half, s_all, s_pair, s_in, k_buf, v_buf, out_buf, s_acc,
+           q_all, o_all, o_pair, o_in, o_half, s_all, s_pair, s_in, k_buf, v_buf, out_buf,
            q_sem, k_sem, v_sem, out_sem, ag_send, ag_recv, pq_send, pq_recv,
            po_send, po_recv, ps_send, ps_recv, rs_send, rs_recv, ss_send, ss_recv):
     half = ring // 2
@@ -107,44 +108,45 @@
         arrived(q_all.at[1, :, area], pq_recv.at[c])
         for copy in load_kv(c):
             copy.wait()
-        s_acc[...] = jnp.zeros_like(s_acc)
-
-        @pl.loop(0, seqs // GROUP)
-        def _(g):
-            first = g * GROUP
-            r0 = pl.multiple_of(c * rows + first * DRAFT, GROUP * DRAFT)
-            q = q_all[:, :, pl.ds(r0, GROUP * DRAFT), :].astype(jnp.float32)
-            q = q.reshape(2, ring, GROUP // 2, 8, head_dim)
-            acc = s_acc[...]
-            outs = []
-            for pair in range(GROUP // 2):
-                mine, theirs = q[0, :, pair], q[1, :, pair]
-                both = (jnp.where(low, mine, pltpu.roll(theirs, DRAFT, 1)), jnp.where(low, pltpu.roll(mine, DRAFT, 1), theirs))
-                pair_out = []
-                for odd in range(2):
-                    local = first + 2 * pair + odd
-                    seq = c * seqs + local
-                    q_rows = both[odd].reshape(ring * 8, head_dim).astype(jnp.bfloat16)
-                    s = lax.dot_general(q_rows, k_buf[seq], (((1,), (1,)), ((), ())), preferred_element_type=jnp.float32)
-                    limit = len_ref[seq] - DRAFT - me * span_len
-                    s = jnp.where((lane_less_token <= limit)[None], s.reshape(ring, 8, span_len), NEG_BIG)
+        acc = jnp.zeros((ring, 8, LANES), jnp.float32)
+        quads = seqs // QUAD
+        scores, probs = {}, {}
+        for step in range(quads + 2 * LAG):
+            if step < quads:
+                r0 = pl.multiple_of(c * rows + step * QUAD * DRAFT, QUAD * DRAFT)
+                q = q_all[:, :, pl.ds(r0, QUAD * DRAFT), :].astype(jnp.float32).reshape(2, ring, QUAD // 2, 8, head_dim)
+                for pair in range(QUAD // 2):
+                    mine, theirs = q[0, :, pair], q[1, :, pair]
+                    both = (jnp.where(low, mine, pltpu.roll(theirs, DRAFT, 1)), jnp.where(low, pltpu.roll(mine, DRAFT, 1), theirs))
+                    for odd in range(2):
+                        local = step * QUAD + 2 * pair + odd
+                        q_rows = both[odd].reshape(ring * 8, head_dim).astype(jnp.bfloat16)
+                        scores[local] = lax.dot_general(q_rows, k_buf[c * seqs + local], (((1,), (1,)), ((), ())),
+                                                        preferred_element_type=jnp.float32)
+            if 0 <= step - LAG < quads:
+                for local in range((step - LAG) * QUAD, (step - LAG + 1) * QUAD):
+                    limit = len_ref[c * seqs + local] - DRAFT - me * span_len
+                    s = scores.pop(local).reshape(ring, 8, span_len)
+                    s = jnp.where((lane_less_token <= limit)[None], s, NEG_BIG)
                     peak = jnp.max(s, axis=2, keepdims=True)
                     p = jnp.exp2((s - peak) * scale)
                     mass = jnp.sum(p, axis=2, keepdims=True)
-                    o = jnp.dot(p.astype(jnp.bfloat16).reshape(ring * 8, span_len), v_buf[seq], preferred_element_type=jnp.float32)
-                    pair_out.append(o.reshape(ring, 8, head_dim) * (1.0 / mass))
-                    log_mass = peak * scale + jnp.log2(mass)
-                    acc = jnp.where((lane_less_token == DRAFT * local)[None], log_mass, acc)
-                even, odd_ = pair_out
-                outs.append((jnp.where(low, even, pltpu.roll(odd_, DRAFT, 1)), jnp.where(low, pltpu.roll(even, DRAFT, 1), odd_)))
-                if pair % 2 == 1:
-                    at = pl.ds(pl.multiple_of(r0 + (pair - 1) * 8, 16), 16)
-                    for side in range(2):
-                        tile = jnp.concatenate([outs[-2][side], outs[-1][side]], axis=1)
-                        o_all[side, :, at, :] = tile.astype(jnp.bfloat16)
-            s_acc[...] = acc
-
-        acc = s_acc[...]
+                    acc = jnp.where((lane_less_token == DRAFT * local)[None], peak * scale + jnp.log2(mass), acc)
+                    probs[local] = (p.astype(jnp.bfloat16).reshape(ring * 8, span_len), 1.0 / mass)
+            if 0 <= step - 2 * LAG < quads:
+                outs = []
+                for local in range((step - 2 * LAG) * QUAD, (step - 2 * LAG + 1) * QUAD):
+                    p, inv = probs.pop(local)
+                    o = jnp.dot(p, v_buf[c * seqs + local], preferred_element_type=jnp.float32)
+                    outs.append(o.reshape(ring, 8, head_dim) * inv)
+                sides = [[], []]
+                for even, odd_ in zip(outs[0::2], outs[1::2]):
+                    sides[0].append(jnp.where(low, even, pltpu.roll(odd_, DRAFT, 1)))
+                    sides[1].append(jnp.where(low, pltpu.roll(even, DRAFT, 1), odd_))
+                at = pl.ds(pl.multiple_of(c * rows + (step - 2 * LAG) * QUAD * DRAFT, QUAD * DRAFT), QUAD * DRAFT)
+                for side in range(2):
+                    o_all[side, :, at, :] = jnp.concatenate(sides[side], axis=1).astype(jnp.bfloat16)
+
         mine = jnp.sum(jnp.where(low, acc, 0.0), axis=1)
         theirs = jnp.sum(jnp.where(low, 0.0, acc), axis=1)
         for slot in range(ring):
@@ -268,7 +270,6 @@
                 pltpu.VMEM(k_span.shape, bf16),
                 pltpu.VMEM(v_span.shape, bf16),
                 pltpu.VMEM((total_rows, head_dim), bf16),
-                pltpu.VMEM((ring, 8, LANES), f32),
                 dma, dma((chunks,)), dma((chunks,)), dma,
                 dma((2, half)), dma((chunks, 2, half)), dma, dma((chunks,)),
                 dma, dma((chunks,)), dma, dma((chunks,)),

time: 125 us -> 67.8 us (0.54)
  Pallas kernels: 123 us -> 65.9 us
    pallas_call x1, Pallas kernels: 123 us -> 65.9 us  [group_step(): pl.pallas_call(functools.partial(kernel, ring), out_shape=jax.ShapeDtypeS...]
where the time goes in v2:
time: 67.8 us; the launch traced here: 67.7 us
  Pallas kernels  65.9 us (97%)
  local copies, waits for them, and re-layouts  1.74 us (3%)
    pallas_call x1, Pallas kernels, group_step(): pl.pallas_call(functools.partial(kernel, ring), out_shape=jax.ShapeDtypeS...  65.9 us
    unnamed x1, local copies, waits for them, and re-layouts  1.74 us

profile of v2, /device:TPU:22, one launch (start us, length us, event | category | flops | bytes accessed | tf_op | source)
XLA Modules:
  0.0 67.7 jit_solution(18418271952992686541)
XLA Ops:
  0.0 65.9 %shard_map.46 = bf16[1024,128]{1,0:T(8,128)(2,1)} custom-call(s32[256]{0:T(256)} %len_ref.1, bf16[1024,128]{1,0:T(8,128)(2,1)} %bitcast.3, bf16[256,128,128]{2,1,0:T(8,128)(2,1)} %k_hbm.1, bf16[256,128,128]{2,1,0:T(8,128)(2,1)} %v_hbm.1), custom_call_target="tpu_custom_call" | custom-call | tf_op jit(solution)/shard_map/pallas_call | solution.py:256
  65.9 1.7 %copy.6 = bf16[256,4,128]{2,1,0:T(4,128)(2,1)} copy(bf16[256,4,128]{2,1,0:T(4,128)(2,1)} %bitcast.2) | data formatting | bytes 524288

commit v3 on v2

--- a/solution.py
+++ b/solution.py
@@ -16,13 +16,13 @@
 MESH_ID = pl.DeviceIdType.MESH
 
 SKEW_GATHER = (0, 2, 4, 6, 8)
-SKEW_COMPUTE = 9
+ORDER = [(0, 0, 5), (0, 0, 3), (0, 0, 7), (0, 0, 6), (0, 0, 2), (0, 1, 5), (0, 1, 3), (0, 1, 7), (0, 0, 4), (0, 0, 1), (0, 2, 5), (0, 0, 0), (0, 2, 3), (0, 1, 6), (0, 1, 4), (0, 3, 5), (0, 2, 7), (0, 1, 2), (0, 1, 1), (0, 2, 6), (0, 3, 3), (0, 4, 5), (0, 2, 4), (0, 3, 7), (0, 1, 0), (0, 2, 2), (1, 0, 5), (0, 3, 6), (0, 2, 1), (0, 4, 3), (2, 4, 5), (0, 4, 7), (0, 3, 4), (1, 0, 3), (0, 2, 0), (0, 3, 2), (0, 4, 6), (1, 0, 7), (0, 3, 1), (0, 4, 4), (2, 4, 3), (2, 3, 5), (1, 0, 6), (0, 3, 0), (2, 4, 7), (0, 4, 2), (1, 0, 4), (2, 4, 6), (2, 3, 3), (0, 4, 1), (1, 0, 2), (2, 3, 7), (2, 4, 4), (2, 2, 5), (0, 4, 0), (1, 0, 1), (2, 4, 2), (2, 2, 3), (2, 3, 6), (1, 0, 0), (2, 4, 1), (2, 3, 4), (2, 2, 7), (2, 4, 0), (2, 1, 5), (2, 3, 2), (2, 3, 1), (2, 2, 6), (2, 3, 0), (2, 2, 4), (2, 2, 2), (2, 2, 1), (2, 1, 3), (2, 2, 0), (2, 1, 4), (2, 1, 6), (2, 1, 1), (2, 0, 5), (2, 1, 2), (2, 1, 0), (2, 1, 7), (2, 0, 1), (2, 0, 6), (2, 0, 3), (2, 0, 4), (2, 0, 2), (2, 0, 0), (2, 0, 7)]
 SKEW_REDUCE = (18, 16, 14, 12, 10)
 
 
-def kernel(ring, len_ref, q_hbm, k_hbm, v_hbm, out_hbm,
-           q_all, o_all, o_pair, o_in, o_half, s_all, s_pair, s_in, k_buf, v_buf, out_buf,
-           q_sem, k_sem, v_sem, out_sem, ag_send, ag_recv, pq_send, pq_recv,
+def kernel(ring, len_ref, q_hbm, k_hbm, v_hbm, out_ref,
+           q_all, o_all, o_pair, o_in, o_half, s_all, s_pair, s_in, k_buf, v_buf,
+           q_sem, k_sem, v_sem, ag_send, ag_recv, pq_send, pq_recv,
            po_send, po_recv, ps_send, ps_recv, rs_send, rs_recv, ss_send, ss_recv):
     half = ring // 2
     num_chunks = s_all.shape[1]
@@ -214,21 +214,15 @@
         if dist == 0:
             cols, _ = weigh([s_all[0, c, 0], s_pair[c, 0], s_in[0, 0, c], s_in[1, 0, c]])
             blocks = [o_all[0, 0, area, :], o_pair[0, area, :], o_in[0, 0, area, :], o_in[1, 0, area, :]]
-            out_buf[area, :] = mix(cols, blocks).astype(jnp.bfloat16)
-            pltpu.make_async_copy(out_buf.at[area], out_hbm.at[area], out_sem).start()
-
-    stages = [(SKEW_GATHER[hop], functools.partial(gather, hop)) for hop in reversed(range(half + 1))]
-    stages += [(SKEW_COMPUTE, compute)]
-    stages += [(SKEW_REDUCE[dist], functools.partial(reduce_hop, dist)) for dist in range(half + 1)]
-
-    @pl.loop(0, num_chunks + max(skew for skew, _ in stages))
-    def _(step):
-        for skew, stage in stages:
-            c = step - skew
-
-            @pl.when(jnp.logical_and(c >= 0, c < num_chunks))
-            def _(stage=stage, c=c):
-                stage(c)
+            out_ref[area, :] = mix(cols, blocks).astype(jnp.bfloat16)
+
+    for kind, hop, c in ORDER:
+        if kind == 0:
+            gather(hop, c)
+        elif kind == 1:
+            compute(c)
+        else:
+            reduce_hop(hop, c)
 
     for way in range(2):
         for hop in range(half):
@@ -239,7 +233,6 @@
     arrived(q_all.at[1], pq_send)
     arrived(o_all.at[1], po_send)
     arrived(s_all.at[1], ps_send)
-    arrived(out_buf, out_sem)
 
 
 def solution(mesh):
@@ -255,9 +248,9 @@
         dma = pltpu.SemaphoreType.DMA
         out = pl.pallas_call(
             functools.partial(kernel, ring),
-            out_shape=jax.ShapeDtypeStruct((total_rows, head_dim), bf16),
+            out_shape=pltpu.VMEM((total_rows, head_dim), bf16),
             in_specs=[pl.BlockSpec(memory_space=pltpu.SMEM)] + [pl.BlockSpec(memory_space=pl.ANY)] * 3,
-            out_specs=pl.BlockSpec(memory_space=pl.ANY),
+            out_specs=pl.BlockSpec(memory_space=pltpu.VMEM),
             scratch_shapes=[
                 pltpu.VMEM((2, ring, total_rows, head_dim), bf16),
                 pltpu.VMEM((2, ring, total_rows, head_dim), bf16),
@@ -269,8 +262,7 @@
                 pltpu.VMEM((2, half, chunks, 1, LANES), f32),
                 pltpu.VMEM(k_span.shape, bf16),
                 pltpu.VMEM(v_span.shape, bf16),
-                pltpu.VMEM((total_rows, head_dim), bf16),
-                dma, dma((chunks,)), dma((chunks,)), dma,
+                dma, dma((chunks,)), dma((chunks,)),
                 dma((2, half)), dma((chunks, 2, half)), dma, dma((chunks,)),
                 dma, dma((chunks,)), dma, dma((chunks,)),
                 dma((2, half)), dma((chunks, 2, half)), dma((2, half)), dma((chunks, 2, half)),

time: 67.8 us -> 60.9 us (0.90)
  the two profiles are of different devices: /device:TPU:22 before, /device:TPU:21 now
where the time goes in v3:
time: 60.9 us; the launch traced here: 60.4 us
  Pallas kernels  59.7 us (98%)
  local copies, waits for them, and re-layouts  0.71 us (1%)
    pallas_call x1, Pallas kernels, group_step(): pl.pallas_call(functools.partial(kernel, ring), out_shape=pltpu.VMEM((tot...  59.7 us

profile of v3, /device:TPU:21, one launch (start us, length us, event | category | flops | bytes accessed | tf_op | source)
XLA Modules:
  0.0 60.4 jit_solution(4784943921226591678)
XLA Ops:
  0.0 59.7 %shard_map.46 = bf16[1024,128]{1,0:T(8,128)(2,1)S(1)} custom-call(s32[256]{0:T(256)} %len_ref.1, bf16[1024,128]{1,0:T(8,128)(2,1)} %bitcast.3, bf16[256,128,128]{2,1,0:T(8,128)(2,1)} %k_hbm.1, bf16[256,128,128]{2,1,0:T(8,128)(2,1)} %v_hbm.1), custom_call_target="tpu_custom_call" | custom-call | tf_op jit(solution)/shard_map/pallas_call | solution.py:249
  59.7 0.7 %copy.6 = bf16[256,4,128]{2,1,0:T(4,128)(2,1)} copy(bf16[256,4,128]{2,1,0:T(4,128)(2,1)S(1)} %bitcast.2) | data formatting | bytes 524288

commit v4 on v3

--- a/solution.py
+++ b/solution.py
@@ -36,8 +36,8 @@
     z = me // 2
     core = lax.rem(me, 2)
     partner = me + 1 - 2 * core
-    right = lax.rem(z + 1, ring) * 2 + core
-    left = lax.rem(z + ring - 1, ring) * 2 + core
+    right = lax.rem(z + 1, ring) * 2 + 1 - core
+    left = lax.rem(z + ring - 1, ring) * 2 + 1 - core
     beside = (right, left)
 
     def load_kv(c):
@@ -188,13 +188,16 @@
             else:
                 arrived(o_in.at[way, dist, area], rs_recv.at[c, way, dist])
             arrived(s_in.at[way, dist, c], ss_recv.at[c, way, dist])
-            if dist == 0:
-                continue
-            slot = dist if way == 0 else ring - dist
+        slots = (dist, ring - dist) if dist else ()
+        weights = []
+        for way, slot in enumerate(slots):
             coming = s_in[way, dist, c]
             if dist == half - 1:
                 coming = jnp.where((row_lane < half_rows) if way == 0 else (row_lane >= half_rows), coming, NEG_BIG)
-            cols, stat = weigh([s_all[0, c, slot], s_pair[c, slot], coming])
+            weights.append(weigh([s_all[0, c, slot], s_pair[c, slot], coming]))
+        for way, slot in enumerate(slots):
+            cols, stat = weights[way]
+            s_all[0, c, slot] = stat
             if dist == half - 1:
                 for part in range(2):
                     at = split_rows(c, part)
@@ -206,7 +209,6 @@
             else:
                 blocks = [o_all[0, slot, area, :], o_pair[slot, area, :], o_in[way, dist, area, :]]
                 o_all[0, slot, area, :] = mix(cols, blocks).astype(jnp.bfloat16)
-            s_all[0, c, slot] = stat
             send(o_all.at[0, slot, area], o_in.at[way, dist - 1, area],
                  rs_send.at[way, dist - 1], rs_recv.at[c, way, dist - 1], beside[way]).start()
             send(s_all.at[0, c, slot], s_in.at[way, dist - 1, c],

time: 60.9 us -> 59.4 us (0.975)
  Pallas kernels: 59.7 us -> 58.6 us
    pallas_call x1, Pallas kernels: 59.7 us -> 58.6 us  [group_step(): pl.pallas_call(functools.partial(kernel, ring), out_shape=pltpu.VMEM((tot...]
where the time goes in v4:
time: 59.4 us; the launch traced here: 59.3 us
  Pallas kernels  58.6 us (99%)
  local copies, waits for them, and re-layouts  0.71 us (1%)
    pallas_call x1, Pallas kernels, group_step(): pl.pallas_call(functools.partial(kernel, ring), out_shape=pltpu.VMEM((tot...  58.6 us

profile of v4, /device:TPU:21, one launch (start us, length us, event | category | flops | bytes accessed | tf_op | source)
XLA Modules:
  0.0 59.3 jit_solution(4739804319488425424)
XLA Ops:
  0.0 58.6 %shard_map.46 = bf16[1024,128]{1,0:T(8,128)(2,1)S(1)} custom-call(s32[256]{0:T(256)} %len_ref.1, bf16[1024,128]{1,0:T(8,128)(2,1)} %bitcast.3, bf16[256,128,128]{2,1,0:T(8,128)(2,1)} %k_hbm.1, bf16[256,128,128]{2,1,0:T(8,128)(2,1)} %v_hbm.1), custom_call_target="tpu_custom_call" | custom-call | tf_op jit(solution)/shard_map/pallas_call | solution.py:251
  58.6 0.7 %copy.6 = bf16[256,4,128]{2,1,0:T(4,128)(2,1)} copy(bf16[256,4,128]{2,1,0:T(4,128)(2,1)S(1)} %bitcast.2) | data formatting | bytes 524288

commit v5 on v4

--- a/solution.py
+++ b/solution.py
@@ -76,26 +76,26 @@
     def half_rows_of(c):
         return pl.ds(pl.multiple_of(c * half_rows, half_rows), half_rows)
 
-    def slot_at(way, hop):
-        return lax.rem(ring - hop, ring) if way == 0 else hop
+    def slot_of(way, dist):
+        return 0 if dist == 0 else ring - 1 if dist == half else 2 * dist - 1 + way
 
     def gather(hop, c):
         area = chunk_rows(c)
-        slots = [(ring - hop) % ring, hop % ring]
+        slots = [slot_of(1 - way, hop) for way in range(2)]
         if 0 < hop < half:
             for way in range(2):
                 arrived(q_all.at[0, slots[way], area], ag_recv.at[c, way, hop - 1])
         elif hop == half:
             for way in range(2):
-                arrived(q_all.at[0, half, split_rows(c, way)], ag_recv.at[c, way, hop - 1])
+                arrived(q_all.at[0, ring - 1, split_rows(c, way)], ag_recv.at[c, way, hop - 1])
         if hop < half:
             for way in range(2):
                 part = area if hop + 1 < half else split_rows(c, way)
-                to = (ring - hop - 1) if way == 0 else hop + 1
+                to = slot_of(1 - way, hop + 1)
                 send(q_all.at[0, slots[way], part], q_all.at[0, to, part],
                      ag_send.at[way, hop], ag_recv.at[c, way, hop], beside[way]).start()
-        for slot in sorted(set(slots)):
-            send(q_all.at[0, slot, area], q_all.at[1, slot, area], pq_send, pq_recv.at[c], partner).start()
+        both = pl.ds(min(slots), len(set(slots)))
+        send(q_all.at[0, both, area], q_all.at[1, both, area], pq_send, pq_recv.at[c], partner).start()
 
     sub = lax.broadcasted_iota(jnp.int32, (8, LANES), 0)
     lane = lax.broadcasted_iota(jnp.int32, (8, LANES), 1)
@@ -173,13 +173,13 @@
         if dist == half:
             arrived(o_pair.at[:, area], po_recv.at[c])
             arrived(s_pair.at[c], ps_recv.at[c])
-            cols, stat = weigh([s_all[0, c, half], s_pair[c, half]])
-            o_all[0, half, area, :] = mix(cols, [o_all[0, half, area, :], o_pair[half, area, :]]).astype(jnp.bfloat16)
-            s_all[0, c, half] = stat
-            for way in range(2):
-                send(o_all.at[0, half, split_rows(c, way)], o_half.at[way, half_rows_of(c)],
+            cols, stat = weigh([s_all[0, c, ring - 1], s_pair[c, ring - 1]])
+            o_all[0, ring - 1, area, :] = mix(cols, [o_all[0, ring - 1, area, :], o_pair[ring - 1, area, :]]).astype(jnp.bfloat16)
+            s_all[0, c, ring - 1] = stat
+            for way in range(2):
+                send(o_all.at[0, ring - 1, split_rows(c, way)], o_half.at[way, half_rows_of(c)],
                      rs_send.at[way, half - 1], rs_recv.at[c, way, half - 1], beside[way]).start()
-                send(s_all.at[0, c, half], s_in.at[way, half - 1, c],
+                send(s_all.at[0, c, ring - 1], s_in.at[way, half - 1, c],
                      ss_send.at[way, half - 1], ss_recv.at[c, way, half - 1], beside[way]).start()
             return
         for way in range(2):
@@ -188,7 +188,7 @@
             else:
                 arrived(o_in.at[way, dist, area], rs_recv.at[c, way, dist])
             arrived(s_in.at[way, dist, c], ss_recv.at[c, way, dist])
-        slots = (dist, ring - dist) if dist else ()
+        slots = (slot_of(0, dist), slot_of(1, dist)) if dist else ()
         weights = []
         for way, slot in enumerate(slots):
             coming = s_in[way, dist, c]
@@ -218,23 +218,26 @@
             blocks = [o_all[0, 0, area, :], o_pair[0, area, :], o_in[0, 0, area, :], o_in[1, 0, area, :]]
             out_ref[area, :] = mix(cols, blocks).astype(jnp.bfloat16)
 
-    for kind, hop, c in ORDER:
+    def sends_done():
+        for way in range(2):
+            for hop in range(half):
+                area = pl.ds(0, num_chunks * (rows if hop + 1 < half else half_rows))
+                arrived(q_all.at[0, hop, area], ag_send.at[way, hop])
+                arrived(o_all.at[0, hop, area], rs_send.at[way, hop])
+                arrived(s_in.at[way, hop], ss_send.at[way, hop])
+        arrived(q_all.at[1], pq_send)
+        arrived(o_all.at[1], po_send)
+        arrived(s_all.at[1], ps_send)
+
+    for at, (kind, hop, c) in enumerate(ORDER):
+        if at == len(ORDER) - 1:
+            sends_done()
         if kind == 0:
             gather(hop, c)
         elif kind == 1:
             compute(c)
         else:
             reduce_hop(hop, c)
-
-    for way in range(2):
-        for hop in range(half):
-            area = pl.ds(0, num_chunks * (rows if hop + 1 < half else half_rows))
-            arrived(q_all.at[0, hop, area], ag_send.at[way, hop])
-            arrived(o_all.at[0, hop, area], rs_send.at[way, hop])
-            arrived(s_in.at[way, hop], ss_send.at[way, hop])
-    arrived(q_all.at[1], pq_send)
-    arrived(o_all.at[1], po_send)
-    arrived(s_all.at[1], ps_send)
 
 
 def solution(mesh):

time: 59.4 us -> 59.3 us (level)
  no operation moved by 1% of the time
where the time goes in v5:
time: 59.3 us; the launch traced here: 59.2 us
  Pallas kernels  58.5 us (99%)
  local copies, waits for them, and re-layouts  0.71 us (1%)
    pallas_call x1, Pallas kernels, group_step(): pl.pallas_call(functools.partial(kernel, ring), out_shape=pltpu.VMEM((tot...  58.5 us

profile of v5, /device:TPU:21, one launch (start us, length us, event | category | flops | bytes accessed | tf_op | source)
XLA Modules:
  0.0 59.2 jit_solution(11315220136796081705)
XLA Ops:
  0.0 58.5 %shard_map.46 = bf16[1024,128]{1,0:T(8,128)(2,1)S(1)} custom-call(s32[256]{0:T(256)} %len_ref.1, bf16[1024,128]{1,0:T(8,128)(2,1)} %bitcast.3, bf16[256,128,128]{2,1,0:T(8,128)(2,1)} %k_hbm.1, bf16[256,128,128]{2,1,0:T(8,128)(2,1)} %v_hbm.1), custom_call_target="tpu_custom_call" | custom-call | tf_op jit(solution)/shard_map/pallas_call | solution.py:254
  58.5 0.7 %copy.6 = bf16[256,4,128]{2,1,0:T(4,128)(2,1)} copy(bf16[256,4,128]{2,1,0:T(4,128)(2,1)S(1)} %bitcast.2) | data formatting | bytes 524288
